TPU v7x, 32 devices: a whole 2x2x4 slice. The times are simulated.
32 devices in a mesh: expert: 32 (over z, y, x, core).
Axes of the slice: x: 2, y: 2, z: 4, core: 2. Of those that a mesh axis runs over, the one named last changes fastest.
Arguments:
- routed_rows: bfloat16 [6144, 2048], P('expert'), may hold values from -6 to 6
- expert_index: int32 [6144, 1], P('expert'), may hold values from 0 to 31; in each aligned block of 192 rows (0 to 191, 192 to 383, ...) at most 12 rows name the same one
- route_weight: float32 [6144], P('expert'), may hold values from 0.1 to 1
- cotangent: bfloat16 [6144, 2048], P('expert'), may hold values from -6 to 6
- gate_weight: bfloat16 [32, 2048, 768], P('expert'), may hold values from -0.125 to 0.125
- up_weight: bfloat16 [32, 2048, 768], P('expert'), may hold values from -0.125 to 0.125
- down_weight: bfloat16 [32, 768, 2048], P('expert'), may hold values from -0.21875 to 0.21875
Outputs:
- layer_out: bfloat16 [6144, 2048], P('expert')
- row_grad: bfloat16 [6144, 2048], P('expert')
- weight_grad: float32 [6144], P('expert')
- gate_grad: bfloat16 [32, 2048, 768], P('expert')
- up_grad: bfloat16 [32, 2048, 768], P('expert')
- down_grad: bfloat16 [32, 768, 2048], P('expert')
Inputs may be any that keep to these rules, and one draw needn't show every extreme that they name: `expert_index`: among the 192 rows of one device no expert is named more than 12 times, a bound that some block reaches.
All inputs are finite; a program needn't handle non-finite values.
Results may differ from a plain program's by a relative error of at most 0.0058.
Values may be sent and summed in bfloat16 or wider, within the bound.
A program may use at most 128 MiB of HBM per device.

v0:
```python
import jax
import jax.numpy as jnp
from jax import lax
from jax.sharding import PartitionSpec as P


def forward_part(rows_in, w_gate, w_up, w_down):
    gate_act = jnp.dot(rows_in, w_gate, preferred_element_type=jnp.float32)
    up_act = jnp.dot(rows_in, w_up, preferred_element_type=jnp.float32)
    sigma = jax.nn.sigmoid(gate_act)
    silu_gate = gate_act * sigma
    hidden = (silu_gate * up_act).astype(jnp.bfloat16)
    expert_out = jnp.dot(hidden, w_down, preferred_element_type=jnp.float32).astype(jnp.bfloat16)
    return (expert_out, (gate_act, up_act, sigma, silu_gate, hidden))


def backward_part(rows_in, out_grad, saved, w_gate, w_up, w_down):
    gate_act, up_act, sigma, silu_gate, hidden = saved
    hidden_grad = lax.dot_general(
        out_grad, w_down, (((1,), (1,)), ((), ())), preferred_element_type=jnp.float32
    )
    gate_pre = (hidden_grad * up_act * sigma * (1.0 + gate_act * (1.0 - sigma))).astype(
        jnp.bfloat16
    )
    up_pre = (hidden_grad * silu_gate).astype(jnp.bfloat16)
    input_grad = (
        lax.dot_general(
            gate_pre, w_gate, (((1,), (1,)), ((), ())), preferred_element_type=jnp.float32
        )
        + lax.dot_general(
            up_pre, w_up, (((1,), (1,)), ((), ())), preferred_element_type=jnp.float32
        )
    ).astype(jnp.bfloat16)
    gate_grad = lax.dot_general(
        rows_in, gate_pre, (((0,), (0,)), ((), ())), preferred_element_type=jnp.float32
    ).astype(jnp.bfloat16)
    up_grad = lax.dot_general(
        rows_in, up_pre, (((0,), (0,)), ((), ())), preferred_element_type=jnp.float32
    ).astype(jnp.bfloat16)
    down_grad = lax.dot_general(
        hidden, out_grad, (((0,), (0,)), ((), ())), preferred_element_type=jnp.float32
    ).astype(jnp.bfloat16)
    return (input_grad, gate_grad, up_grad, down_grad)


def local(routed_rows, expert_index, route_weight, cotangent, gate_weight, up_weight, down_weight):
    devices = lax.axis_size("expert")
    row_count = routed_rows.shape[0]
    width = routed_rows.shape[1]
    capacity = max(2, 2 * row_count // devices)
    choice_ids = expert_index[:, 0]
    onehot = (choice_ids[:, None] == jnp.arange(devices, dtype=jnp.int32)[None, :]).astype(
        jnp.float32
    )
    earlier = (jnp.arange(row_count)[:, None] > jnp.arange(row_count)[None, :]).astype(jnp.float32)
    before = jnp.dot(earlier, onehot, preferred_element_type=jnp.float32)
    rank_within = jnp.sum(before * onehot, axis=1).astype(jnp.int32)
    slot_index = choice_ids * capacity + rank_within
    scatter_table = (
        jnp.arange(devices * capacity, dtype=jnp.int32)[:, None] == slot_index[None, :]
    ).astype(jnp.bfloat16)
    out_grad = (route_weight[:, None] * cotangent.astype(jnp.float32)).astype(jnp.bfloat16)
    send_rows = jnp.dot(scatter_table, routed_rows, preferred_element_type=jnp.float32).astype(
        jnp.bfloat16
    )
    send_rows = send_rows.reshape(devices, capacity, width)
    send_grad = jnp.dot(scatter_table, out_grad, preferred_element_type=jnp.float32).astype(
        jnp.bfloat16
    )
    send_grad = send_grad.reshape(devices, capacity, width)
    w_gate = gate_weight[0]
    w_up = up_weight[0]
    w_down = down_weight[0]
    got_rows = lax.all_to_all(send_rows, "expert", split_axis=0, concat_axis=0, tiled=True)
    rows_in = got_rows.reshape(devices * capacity, width)
    expert_out, saved = forward_part(rows_in, w_gate, w_up, w_down)
    back_out = lax.all_to_all(
        expert_out.reshape(devices, capacity, width),
        "expert",
        split_axis=0,
        concat_axis=0,
        tiled=True,
    )
    got_grad = lax.all_to_all(send_grad, "expert", split_axis=0, concat_axis=0, tiled=True)
    input_grad, gate_grad, up_grad, down_grad = backward_part(
        rows_in, got_grad.reshape(devices * capacity, width), saved, w_gate, w_up, w_down
    )
    back_grad = lax.all_to_all(
        input_grad.reshape(devices, capacity, width),
        "expert",
        split_axis=0,
        concat_axis=0,
        tiled=True,
    )
    gather_dims = (((0,), (0,)), ((), ()))
    out_rows = lax.dot_general(
        scatter_table,
        back_out.reshape(devices * capacity, width),
        gather_dims,
        preferred_element_type=jnp.float32,
    ).astype(jnp.bfloat16)
    row_grad = lax.dot_general(
        scatter_table,
        back_grad.reshape(devices * capacity, width),
        gather_dims,
        preferred_element_type=jnp.float32,
    ).astype(jnp.bfloat16)
    layer_out = (route_weight[:, None] * out_rows.astype(jnp.float32)).astype(jnp.bfloat16)
    weight_grad = jnp.sum(cotangent.astype(jnp.float32) * out_rows.astype(jnp.float32), axis=1)
    return (layer_out, row_grad, weight_grad, gate_grad[None], up_grad[None], down_grad[None])


def solution(mesh):
    return jax.shard_map(
        local,
        mesh=mesh,
        in_specs=(
            P("expert", None),
            P("expert", None),
            P("expert"),
            P("expert", None),
            P("expert", None, None),
            P("expert", None, None),
            P("expert", None, None),
        ),
        out_specs=(
            P("expert", None),
            P("expert", None),
            P("expert"),
            P("expert", None, None),
            P("expert", None, None),
            P("expert", None, None),
        ),
        check_vma=False,
    )
```

profile of v0, /device:TPU:0, one launch (start us, length us, event | category | flops | bytes accessed | tf_op | source)
XLA Modules:
  0.0 247.9 jit_solution(11534408576833595987)
XLA Ops:
  2.4 2.9 %convolution_convert_fusion.3 = bf16[384,2048]{1,0:T(8,128)(2,1)} fusion(bf16[192,2048]{1,0:T(8,128)(2,1)} %param.10, f32[192]{0:T(256)} %param.9, s32[192]{0:T(256)S(1)} %convert_add_fusion), kind=kOutput, calls=%fused_computation.20 | convolution fusion | flops 304029696 | bytes 2360832 | tf_op jit(solution)/shard_map/dot_general | solution.py:67
  5.3 3.6 %reshape.50 = bf16[32,12,2048]{2,1,0:T(8,128)(2,1)} reshape(bf16[384,2048]{1,0:T(8,128)(2,1)} %convolution_convert_fusion.3) | data formatting | bytes 3145728 | tf_op jit(solution)/shard_map/reshape | solution.py:70
  8.9 7.5 %all-to-all-start.2 = ((bf16[32,12,2048]{2,1,0:T(8,128)(2,1)}), bf16[32,12,2048]{2,1,0:T(8,128)(2,1)}, u32[]{:S(2)}, u32[]{:S(2)}) async-start(bf16[32,12,2048]{2,1,0:T(8,128)(2,1)} %reshape.50), calls=%async_computation.2 | async-start | bytes 4194304 | tf_op jit(solution)/shard_map/all_to_all | solution.py:84
  19.2 3.6 %reshape.46 = bf16[32,12,2048]{2,1,0:T(8,128)(2,1)} reshape(bf16[384,2048]{1,0:T(8,128)(2,1)} %convolution_convert_fusion.4) | data formatting | bytes 3145728 | tf_op jit(solution)/shard_map/reshape | solution.py:66
  22.8 42.3 %all-to-all-done.2 = bf16[32,12,2048]{2,1,0:T(8,128)(2,1)} async-done(((bf16[32,12,2048]{2,1,0:T(8,128)(2,1)}), bf16[32,12,2048]{2,1,0:T(8,128)(2,1)}, u32[]{:S(2)}, u32[]{:S(2)}) %all-to-all-start.2) | async-done | bytes 1572896 | tf_op jit(solution)/shard_map/all_to_all | solution.py:84
  65.1 4.2 %all-to-all-start = ((bf16[32,12,2048]{2,1,0:T(8,128)(2,1)}), bf16[32,12,2048]{2,1,0:T(8,128)(2,1)}, u32[]{:S(2)}, u32[]{:S(2)}) async-start(bf16[32,12,2048]{2,1,0:T(8,128)(2,1)} %reshape.46), calls=%async_computation | async-start | bytes 4194304 | tf_op jit(solution)/shard_map/all_to_all | solution.py:74
  69.3 3.6 %reshape.51 = bf16[384,2048]{1,0:T(8,128)(2,1)} reshape(bf16[32,12,2048]{2,1,0:T(8,128)(2,1)} %all-to-all-done.2) | data formatting | bytes 3145728 | tf_op jit(solution)/shard_map/reshape | solution.py:86
  72.9 4.8 %fusion = f32[384,768]{1,0:T(8,128)} fusion(bf16[384,2048]{1,0:T(8,128)(2,1)} %reshape.51, bf16[1,768,2048]{2,1,0:T(8,128)(2,1)} %param.13), kind=kOutput, calls=%fused_computation.3 | convolution fusion | flops 1207959552 | bytes 5898240 | tf_op jit(solution)/shard_map/dot_general | solution.py:19
  77.7 40.3 %all-to-all-done = bf16[32,12,2048]{2,1,0:T(8,128)(2,1)} async-done(((bf16[32,12,2048]{2,1,0:T(8,128)(2,1)}), bf16[32,12,2048]{2,1,0:T(8,128)(2,1)}, u32[]{:S(2)}, u32[]{:S(2)}) %all-to-all-start) | async-done | bytes 1572896 | tf_op jit(solution)/shard_map/all_to_all | solution.py:74
  118.0 3.6 %reshape.47 = bf16[384,2048]{1,0:T(8,128)(2,1)} reshape(bf16[32,12,2048]{2,1,0:T(8,128)(2,1)} %all-to-all-done) | data formatting | bytes 3145728 | tf_op jit(solution)/shard_map/reshape | solution.py:75
  121.6 3.9 %fusion.6 = f32[384,768]{1,0:T(8,128)S(1)} fusion(bf16[384,2048]{1,0:T(8,128)(2,1)} %reshape.47, bf16[1,2048,768]{2,1,0:T(8,128)(2,1)} %param.12), kind=kOutput, calls=%fused_computation.9 | convolution fusion | flops 1207959552 | bytes 5898240 | tf_op jit(solution)/shard_map/dot_general | solution.py:9
  131.8 3.6 %reshape.48 = bf16[32,12,2048]{2,1,0:T(8,128)(2,1)} reshape(bf16[384,2048]{1,0:T(8,128)(2,1)} %fusion.17) | data formatting | bytes 3145728 | tf_op jit(solution)/shard_map/reshape | solution.py:78
  135.4 4.2 %all-to-all-start.1 = ((bf16[32,12,2048]{2,1,0:T(8,128)(2,1)}), bf16[32,12,2048]{2,1,0:T(8,128)(2,1)}, u32[]{:S(2)}, u32[]{:S(2)}) async-start(bf16[32,12,2048]{2,1,0:T(8,128)(2,1)} %reshape.48), calls=%async_computation.1 | async-start | bytes 4194304 | tf_op jit(solution)/shard_map/all_to_all | solution.py:77
  139.6 3.5 %fusion.4 = f32[384,2048]{1,0:T(8,128)S(1)} fusion(bf16[384,768]{1,0:T(8,128)(2,1)} %get-tuple-element.7, bf16[1,2048,768]{2,1,0:T(8,128)(2,1)} %param.12), kind=kOutput, calls=%fused_computation.7 | convolution fusion | flops 1207959552 | bytes 6881280 | tf_op jit(solution)/shard_map/dot_general | solution.py:30
  145.7 3.6 %reshape.52 = bf16[32,12,2048]{2,1,0:T(8,128)(2,1)} reshape(bf16[384,2048]{1,0:T(8,128)(2,1)} %add_convert_fusion) | data formatting | bytes 3145728 | tf_op jit(solution)/shard_map/reshape | solution.py:89
  149.3 39.0 %all-to-all-done.1 = bf16[32,12,2048]{2,1,0:T(8,128)(2,1)} async-done(((bf16[32,12,2048]{2,1,0:T(8,128)(2,1)}), bf16[32,12,2048]{2,1,0:T(8,128)(2,1)}, u32[]{:S(2)}, u32[]{:S(2)}) %all-to-all-start.1) | async-done | bytes 1572896 | tf_op jit(solution)/shard_map/all_to_all | solution.py:77
  188.3 4.4 %all-to-all-start.3 = ((bf16[32,12,2048]{2,1,0:T(8,128)(2,1)}), bf16[32,12,2048]{2,1,0:T(8,128)(2,1)}, u32[]{:S(2)}, u32[]{:S(2)}) async-start(bf16[32,12,2048]{2,1,0:T(8,128)(2,1)} %reshape.52), calls=%async_computation.3 | async-start | bytes 4194304 | tf_op jit(solution)/shard_map/all_to_all | solution.py:88
  192.8 5.2 %fusion.12 = bf16[1,2048,768]{2,1,0:T(8,128)(2,1)} fusion(bf16[384,2048]{1,0:T(8,128)(2,1)} %reshape.47, bf16[384,768]{1,0:T(8,128)(2,1)} %get-tuple-element.6), kind=kOutput, calls=%fused_computation.16 | convolution fusion | flops 1209532416 | bytes 5308416 | tf_op jit(solution)/shard_map/dot_general | solution.py:34
  198.0 3.5 %fusion.13 = bf16[1,2048,768]{2,1,0:T(8,128)(2,1)} fusion(bf16[384,2048]{1,0:T(8,128)(2,1)S(1)} %copy-done.3, bf16[384,768]{1,0:T(8,128)(2,1)S(1)} %copy-done.8), kind=kOutput, calls=%fused_computation.17 | convolution fusion | flops 1209532416 | bytes 5308416 | tf_op jit(solution)/shard_map/dot_general | solution.py:37
  201.5 3.5 %fusion.14 = bf16[1,768,2048]{2,1,0:T(8,128)(2,1)} fusion(bf16[384,768]{1,0:T(8,128)(2,1)S(1)} %copy-done.10, bf16[384,2048]{1,0:T(8,128)(2,1)S(1)} %copy-done.1), kind=kOutput, calls=%fused_computation.18 | convolution fusion | flops 1209532416 | bytes 5308416 | tf_op jit(solution)/shard_map/dot_general | solution.py:40
  205.0 3.6 %reshape.49 = bf16[384,2048]{1,0:T(8,128)(2,1)} reshape(bf16[32,12,2048]{2,1,0:T(8,128)(2,1)} %all-to-all-done.1) | data formatting | bytes 3145728 | tf_op jit(solution)/shard_map/reshape | solution.py:98
  208.6 3.8 %fusion.22 = (f32[192]{0:T(256)}, bf16[192,2048]{1,0:T(8,128)(2,1)}) fusion(bf16[192,2048]{1,0:T(8,128)(2,1)} %param.10, f32[192]{0:T(256)S(1)} %copy-done.4, bf16[384,2048]{1,0:T(8,128)(2,1)} %reshape.49, s32[192]{0:T(256)S(1)} %convert_add_fusion), kind=kOutput, calls=%fused_computation.28 | convolution fusion | flops 304815936 | bytes 3148032 | tf_op jit(solution)/shard_map/dot_general | solution.py:96
  212.4 29.0 %all-to-all-done.3 = bf16[32,12,2048]{2,1,0:T(8,128)(2,1)} async-done(((bf16[32,12,2048]{2,1,0:T(8,128)(2,1)}), bf16[32,12,2048]{2,1,0:T(8,128)(2,1)}, u32[]{:S(2)}, u32[]{:S(2)}) %all-to-all-start.3) | async-done | bytes 1572896 | tf_op jit(solution)/shard_map/all_to_all | solution.py:88
  241.4 3.6 %reshape.53 = bf16[384,2048]{1,0:T(8,128)(2,1)} reshape(bf16[32,12,2048]{2,1,0:T(8,128)(2,1)} %all-to-all-done.3) | data formatting | bytes 3145728 | tf_op jit(solution)/shard_map/reshape | solution.py:104
  (29 shorter events, 16.3 us)
Async XLA Ops:
  0.6 124.9 %copy-start = (bf16[1,2048,768]{2,1,0:T(8,128)(2,1)S(1)}, bf16[1,2048,768]{2,1,0:T(8,128)(2,1)}, u32[]{:S(2)}) copy-start(bf16[1,2048,768]{2,1,0:T(8,128)(2,1)} %param.11) | copy-start | bytes 9437188
  8.9 56.2 %all-to-all-start.2 = ((bf16[32,12,2048]{2,1,0:T(8,128)(2,1)}), bf16[32,12,2048]{2,1,0:T(8,128)(2,1)}, u32[]{:S(2)}, u32[]{:S(2)}) async-start(bf16[32,12,2048]{2,1,0:T(8,128)(2,1)} %reshape.50), calls=%async_computation.2 | async-start | bytes 4194304 | tf_op jit(solution)/shard_map/all_to_all | solution.py:84
  65.1 52.9 %all-to-all-start = ((bf16[32,12,2048]{2,1,0:T(8,128)(2,1)}), bf16[32,12,2048]{2,1,0:T(8,128)(2,1)}, u32[]{:S(2)}, u32[]{:S(2)}) async-start(bf16[32,12,2048]{2,1,0:T(8,128)(2,1)} %reshape.46), calls=%async_computation | async-start | bytes 4194304 | tf_op jit(solution)/shard_map/all_to_all | solution.py:74
  121.6 3.9 %copy-start.2 = (bf16[384,2048]{1,0:T(8,128)(2,1)S(1)}, bf16[384,2048]{1,0:T(8,128)(2,1)}, u32[]{:S(2)}) copy-start(bf16[384,2048]{1,0:T(8,128)(2,1)} %reshape.47) | copy-start | bytes 4718596
  121.6 3.9 %copy-start.7 = (f32[384,768]{1,0:T(8,128)S(1)}, f32[384,768]{1,0:T(8,128)}, u32[]{:S(2)}) copy-start(f32[384,768]{1,0:T(8,128)} %fusion) | copy-start | bytes 3538948
  125.5 3.7 %copy-start.5 = (bf16[1,768,2048]{2,1,0:T(8,128)(2,1)S(1)}, bf16[1,768,2048]{2,1,0:T(8,128)(2,1)}, u32[]{:S(2)}) copy-start(bf16[1,768,2048]{2,1,0:T(8,128)(2,1)} %param.13) | copy-start | bytes 9437188
  128.4 0.9 copy-start.9
  135.4 52.9 %all-to-all-start.1 = ((bf16[32,12,2048]{2,1,0:T(8,128)(2,1)}), bf16[32,12,2048]{2,1,0:T(8,128)(2,1)}, u32[]{:S(2)}, u32[]{:S(2)}) async-start(bf16[32,12,2048]{2,1,0:T(8,128)(2,1)} %reshape.48), calls=%async_computation.1 | async-start | bytes 4194304 | tf_op jit(solution)/shard_map/all_to_all | solution.py:77
  139.6 3.6 %copy-start.6 = (bf16[384,768]{1,0:T(8,128)(2,1)S(1)}, bf16[384,768]{1,0:T(8,128)(2,1)}, u32[]{:S(2)}) copy-start(bf16[384,768]{1,0:T(8,128)(2,1)} %get-tuple-element.6) | copy-start | bytes 1769476
  188.3 53.1 %all-to-all-start.3 = ((bf16[32,12,2048]{2,1,0:T(8,128)(2,1)}), bf16[32,12,2048]{2,1,0:T(8,128)(2,1)}, u32[]{:S(2)}, u32[]{:S(2)}) async-start(bf16[32,12,2048]{2,1,0:T(8,128)(2,1)} %reshape.52), calls=%async_computation.3 | async-start | bytes 4194304 | tf_op jit(solution)/shard_map/all_to_all | solution.py:88
  192.7 5.2 %copy-start.3 = (bf16[384,2048]{1,0:T(8,128)(2,1)S(1)}, bf16[384,2048]{1,0:T(8,128)(2,1)}, u32[]{:S(2)}) copy-start(bf16[384,2048]{1,0:T(8,128)(2,1)} %reshape.47) | copy-start | bytes 4718596
  192.7 5.2 %copy-start.8 = (bf16[384,768]{1,0:T(8,128)(2,1)S(1)}, bf16[384,768]{1,0:T(8,128)(2,1)}, u32[]{:S(2)}) copy-start(bf16[384,768]{1,0:T(8,128)(2,1)} %get-tuple-element.7) | copy-start | bytes 1769476
  197.9 3.5 %copy-start.1 = (bf16[384,2048]{1,0:T(8,128)(2,1)S(1)}, bf16[384,2048]{1,0:T(8,128)(2,1)}, u32[]{:S(2)}) copy-start(bf16[384,2048]{1,0:T(8,128)(2,1)} %reshape.51) | copy-start | bytes 4718596
  198.0 3.5 %copy-start.10 = (bf16[384,768]{1,0:T(8,128)(2,1)S(1)}, bf16[384,768]{1,0:T(8,128)(2,1)}, u32[]{:S(2)}) copy-start(bf16[384,768]{1,0:T(8,128)(2,1)} %copy-done.9) | copy-start | bytes 1769476
  205.0 3.6 %copy-start.4 = (f32[192]{0:T(256)S(1)}, f32[192]{0:T(256)}, u32[]{:S(2)}) copy-start(f32[192]{0:T(256)} %param.9) | copy-start | bytes 2308
where the time goes:
time: 249 us; the launch traced here: 248 us
  waiting for transfers between devices  151 us (61%)
  matrix products  45.9 us (18%)
  local copies, waits for them, and re-layouts  29.7 us (12%)
  starting transfers between devices  20.3 us (8%)
    all_to_all x1, waiting for transfers between devices, local(): lax.all_to_all(send_grad, 'expert', split_axis=0, concat_axis=0, tiled=True)  42.3 us
    all_to_all x1, waiting for transfers between devices, local(): lax.all_to_all(send_rows, 'expert', split_axis=0, concat_axis=0, tiled=True)  40.3 us
    all_to_all x1, waiting for transfers between devices, local(): lax.all_to_all(expert_out.reshape(devices, capacity, width), 'expert', sp...  39 us
    all_to_all x1, waiting for transfers between devices, local(): lax.all_to_all(input_grad.reshape(devices, capacity, width), 'expert', sp...  29 us
    all_to_all x1, starting transfers between devices, local(): lax.all_to_all(send_grad, 'expert', split_axis=0, concat_axis=0, tiled=True)  7.46 us
    dot_general x1, matrix products, backward_part(): lax.dot_general(rows_in, gate_pre, (((0,), (0,)), ((), ())), preferred_el...  5.19 us
  transfers between devices with their start and end apart: 4, of which 4 were waited for; matrix products, arithmetic and copies ran while one was open for 18% of the time, Pallas kernels for 0%

commit v1 on v0

v1 whole, which is shorter than its diff:
```python
import functools
import math

import jax
import jax.numpy as jnp
from jax import lax
from jax.experimental import pallas as pl
from jax.experimental.pallas import tpu as pltpu
from jax.sharding import PartitionSpec as P

F32 = jnp.float32
BF16 = jnp.bfloat16
SUB = 16
NT = (((1,), (1,)), ((), ()))
TN = (((0,), (0,)), ((), ()))


def dot(a, b):
    return jnp.dot(a, b, preferred_element_type=F32)


def kernel(
    n, cap, part, tile,
    idx_row, idx_col, weight_col, rows, cot, wg_any, wu_any, wd_any,
    layer, row_grad, weight_grad, rin_any, og_any, hid_any, gp_any, up_any,
    wg, wu, wd, send, recv, rin, og, ga, ua, hid, gp, up, eo,
    load_sem, store_sem, send_sem, recv_sem, own_sem,
):
    me = lax.axis_index("expert")
    groups = SUB // part
    blocks = cap // part
    row_count, width = rows.shape
    chunk = width // groups
    some = math.gcd(n, 32)
    wide = some * SUB
    narrow = some * part
    hidden_units = wg.shape[1]

    loads = [
        pltpu.make_async_copy(src, dst, load_sem.at[i])
        for i, (src, dst) in enumerate(((wg_any, wg), (wu_any, wu), (wd_any, wd)))
    ]
    for load in loads:
        load.start()

    barrier = pltpu.get_barrier_semaphore()

    @pl.loop(1, n)
    def _(s):
        pl.semaphore_signal(
            barrier, inc=1, device_id=(lax.rem(me + s, n),), device_id_type=pl.DeviceIdType.MESH
        )

    choice_row = idx_row[...]
    hot_row = (lax.broadcasted_iota(jnp.int32, (n, row_count), 0) == choice_row).astype(F32)
    before = (
        lax.broadcasted_iota(jnp.int32, (row_count, row_count), 0)
        < lax.broadcasted_iota(jnp.int32, (row_count, row_count), 1)
    ).astype(F32)
    rank_row = jnp.sum(dot(hot_row, before) * hot_row, axis=0, keepdims=True).astype(jnp.int32)
    choice_col = idx_col[...]
    hot_col = (lax.broadcasted_iota(jnp.int32, (row_count, n), 1) == choice_col).astype(F32)
    after = (
        lax.broadcasted_iota(jnp.int32, (row_count, row_count), 0)
        > lax.broadcasted_iota(jnp.int32, (row_count, row_count), 1)
    ).astype(F32)
    rank_col = jnp.sum(dot(after, hot_col) * hot_col, axis=1, keepdims=True).astype(jnp.int32)

    def place(choice, rank, q):
        off = rank - q * part
        return jnp.where((off >= 0) & (off < part), choice * SUB + off, -SUB * n)

    def columns(c):
        return slice(c * chunk, (c + 1) * chunk)

    def dispatch(p, source):
        @pl.loop(0, n // some)
        def _(b):
            at = pl.ds(pl.multiple_of(b * wide, wide), wide)
            for q in range(blocks):
                base = place(choice_row, rank_row, q) - b * wide
                total = None
                for c in range(groups):
                    table = (
                        lax.broadcasted_iota(jnp.int32, (wide, row_count), 0) == base + c * part
                    ).astype(F32).astype(BF16)
                    term = dot(table, source(c))
                    total = term if total is None else total + term
                send[p, at, columns(q)] = total.astype(BF16)

    def slab(d):
        return pl.ds(pl.multiple_of(d * SUB, SUB), SUB)

    def ship(p):
        own = pltpu.make_async_copy(
            send.at[p, slab(me)], recv.at[p, slab(me)], own_sem.at[p]
        )

        @pl.loop(0, n)
        def _(s):
            to = lax.rem(me + n // 2 + s, n)

            @pl.when(to != me)
            def _():
                pltpu.make_async_remote_copy(
                    src_ref=send.at[p, slab(to)],
                    dst_ref=recv.at[p, slab(me)],
                    send_sem=send_sem.at[p],
                    recv_sem=recv_sem.at[p],
                    device_id=(to,),
                    device_id_type=pl.DeviceIdType.MESH,
                ).start()

        own.start()
        return own

    def arrived(p, own):
        own.wait()
        most = recv.at[p, pl.ds(0, (n - 1) * SUB)]
        pltpu.make_async_copy(most, most, recv_sem.at[p]).wait()

    def left(p):
        most = send.at[p, pl.ds(0, (n - 1) * SUB)]
        pltpu.make_async_copy(most, most, send_sem.at[p]).wait()

    def pick(c):
        row = lax.broadcasted_iota(jnp.int32, (narrow, wide), 0)
        col = lax.broadcasted_iota(jnp.int32, (narrow, wide), 1)
        low = row & (part - 1)
        return (col == (row - low) * groups + c * part + low).astype(F32).astype(BF16)

    def spread(c):
        row = lax.broadcasted_iota(jnp.int32, (wide, narrow), 0)
        col = lax.broadcasted_iota(jnp.int32, (wide, narrow), 1)
        low = col & (part - 1)
        return (row == (col - low) * groups + c * part + low).astype(F32).astype(BF16)

    def unpack(p, into):
        @pl.loop(0, n // some)
        def _(b):
            at = pl.ds(pl.multiple_of(b * wide, wide), wide)
            for c in range(groups):
                table = pick(c)
                for q in range(blocks):
                    to = pl.ds(pl.multiple_of(q * n * part + b * narrow, narrow), narrow)
                    into[to, columns(c)] = dot(table, recv[p, at, columns(q)]).astype(BF16)

    def pack(p):
        @pl.loop(0, n // some)
        def _(b):
            at = pl.ds(pl.multiple_of(b * wide, wide), wide)
            for q in range(blocks):
                to = pl.ds(pl.multiple_of(q * n * part + b * narrow, narrow), narrow)
                total = None
                for c in range(groups):
                    term = dot(spread(c), eo[to, columns(c)])
                    total = term if total is None else total + term
                send[p, at, columns(q)] = total.astype(BF16)

    def combine(p, c):
        total = None
        for b in range(n // some):
            for q in range(blocks):
                base = place(choice_col, rank_col, q) + c * part - b * wide
                table = (
                    lax.broadcasted_iota(jnp.int32, (row_count, wide), 1) == base
                ).astype(F32).astype(BF16)
                term = dot(table, recv[p, b * wide:(b + 1) * wide, columns(q)])
                total = term if total is None else total + term
        return total

    weight = weight_col[...]
    dispatch(0, lambda c: rows[:, columns(c)])
    pl.semaphore_wait(barrier, n - 1)
    own_a = ship(0)
    dispatch(1, lambda c: (weight * cot[:, columns(c)].astype(F32)).astype(BF16))
    own_b = ship(1)
    for load in loads:
        load.wait()

    arrived(0, own_a)
    unpack(0, rin)

    @pl.loop(0, hidden_units // tile)
    def _(t):
        at = pl.ds(pl.multiple_of(t * tile, tile), tile)
        gate = dot(rin[...], wg[:, at])
        upper = dot(rin[...], wu[:, at])
        ga[:, at] = gate
        ua[:, at] = upper
        hid[:, at] = (gate * jax.nn.sigmoid(gate) * upper).astype(BF16)

    @pl.loop(0, width // tile)
    def _(t):
        at = pl.ds(pl.multiple_of(t * tile, tile), tile)
        eo[:, at] = dot(hid[...], wd[:, at]).astype(BF16)

    pack(2)
    own_c = ship(2)

    arrived(1, own_b)
    unpack(1, og)

    @pl.loop(0, hidden_units // tile)
    def _(t):
        at = pl.ds(pl.multiple_of(t * tile, tile), tile)
        grad = lax.dot_general(og[...], wd[at, :], NT, preferred_element_type=F32)
        gate = ga[:, at]
        sigma = jax.nn.sigmoid(gate)
        gp[:, at] = (grad * ua[:, at] * sigma * (1.0 + gate * (1.0 - sigma))).astype(BF16)
        up[:, at] = (grad * (gate * sigma)).astype(BF16)

    @pl.loop(0, width // tile)
    def _(t):
        at = pl.ds(pl.multiple_of(t * tile, tile), tile)
        eo[:, at] = (
            lax.dot_general(gp[...], wg[at, :], NT, preferred_element_type=F32)
            + lax.dot_general(up[...], wu[at, :], NT, preferred_element_type=F32)
        ).astype(BF16)

    pack(3)
    own_d = ship(3)

    stores = [
        pltpu.make_async_copy(src, dst, store_sem.at[i])
        for i, (src, dst) in enumerate(
            ((rin, rin_any), (og, og_any), (hid, hid_any), (gp, gp_any), (up, up_any))
        )
    ]
    for store in stores:
        store.start()

    arrived(2, own_c)
    weight_grad[...] = jnp.zeros_like(weight_grad)

    @pl.loop(0, groups)
    def _(c):
        at = pl.ds(pl.multiple_of(c * chunk, chunk), chunk)
        got = combine(2, c)
        layer[:, at] = (weight * got).astype(BF16)
        weight_grad[...] += jnp.sum(cot[:, at].astype(F32) * got, axis=1, keepdims=True)

    for store in stores:
        store.wait()
    for p in range(3):
        left(p)
    arrived(3, own_d)

    @pl.loop(0, groups)
    def _(c):
        at = pl.ds(pl.multiple_of(c * chunk, chunk), chunk)
        row_grad[:, at] = combine(3, c).astype(BF16)

    left(3)


def local(routed_rows, expert_index, route_weight, cotangent, gate_weight, up_weight, down_weight):
    n = lax.axis_size("expert")
    row_count, width = routed_rows.shape
    units = gate_weight.shape[2]
    cap = max(2, 2 * row_count // n)
    part = math.gcd(cap, SUB)
    slab_width = (cap // part) * (width // (SUB // part))
    slots = n * cap
    tile = math.gcd(256, math.gcd(units, width))
    vmem = pl.BlockSpec(memory_space=pltpu.VMEM)
    hbm = pl.BlockSpec(memory_space=pl.ANY)
    shape = jax.ShapeDtypeStruct
    layer_out, row_grad, weight_grad, rows_in, out_grad, hidden, gate_pre, up_pre = pl.pallas_call(
        functools.partial(kernel, n, cap, part, tile),
        out_shape=(
            shape((row_count, width), BF16),
            shape((row_count, width), BF16),
            shape((row_count, 1), F32),
            shape((slots, width), BF16),
            shape((slots, width), BF16),
            shape((slots, units), BF16),
            shape((slots, units), BF16),
            shape((slots, units), BF16),
        ),
        in_specs=[vmem] * 5 + [hbm] * 3,
        out_specs=(vmem,) * 3 + (hbm,) * 5,
        scratch_shapes=[
            pltpu.VMEM((width, units), BF16),
            pltpu.VMEM((width, units), BF16),
            pltpu.VMEM((units, width), BF16),
            pltpu.VMEM((4, n * SUB, slab_width), BF16),
            pltpu.VMEM((4, n * SUB, slab_width), BF16),
            pltpu.VMEM((slots, width), BF16),
            pltpu.VMEM((slots, width), BF16),
            pltpu.VMEM((slots, units), F32),
            pltpu.VMEM((slots, units), F32),
            pltpu.VMEM((slots, units), BF16),
            pltpu.VMEM((slots, units), BF16),
            pltpu.VMEM((slots, units), BF16),
            pltpu.VMEM((slots, width), BF16),
            pltpu.SemaphoreType.DMA((3,)),
            pltpu.SemaphoreType.DMA((5,)),
            pltpu.SemaphoreType.DMA((4,)),
            pltpu.SemaphoreType.DMA((4,)),
            pltpu.SemaphoreType.DMA((4,)),
        ],
        compiler_params=pltpu.CompilerParams(
            collective_id=0, has_side_effects=True, vmem_limit_bytes=60 * 1024 * 1024
        ),
        name="routed",
    )(
        expert_index.reshape(1, row_count), expert_index, route_weight[:, None], routed_rows,
        cotangent, gate_weight[0], up_weight[0], down_weight[0],
    )
    grads = [
        lax.dot_general(a, b, TN, preferred_element_type=F32).astype(BF16)
        for a, b in ((rows_in, gate_pre), (rows_in, up_pre), (hidden, out_grad))
    ]
    return (layer_out, row_grad, weight_grad[:, 0]) + tuple(g[None] for g in grads)


def solution(mesh):
    rows, vector, cube = P("expert", None), P("expert"), P("expert", None, None)
    return jax.shard_map(
        local,
        mesh=mesh,
        in_specs=(rows, rows, vector, rows, cube, cube, cube),
        out_specs=(rows, rows, vector, cube, cube, cube),
        check_vma=False,
    )
```

time: 249 us -> 168 us (0.67)
  waiting for transfers between devices: 151 us -> 0 us
  Pallas kernels: 0 us -> 149 us
  matrix products: 45.9 us -> 12.2 us
  local copies, waits for them, and re-layouts: 29.7 us -> 4.66 us
  starting transfers between devices: 20.3 us -> 0 us
    all_to_all x4 -> x0, waiting for transfers between devices: 151 us -> none  [the longest x1 42.3 us: local(): lax.all_to_all(send_grad, 'expert', split_axis=0, concat_axis=0, tiled=True)]
    pallas_call x0 -> x1, Pallas kernels: none -> 149 us  [local(): pl.pallas_call(functools.partial(kernel, n, cap, part, tile), out_shape=(...]
    dot_general x14 -> x3, matrix products: 45.9 us -> 12.2 us  [local(): lax.dot_general(a, b, TN, preferred_element_type=F32).astype(BF16)]
    reshape x8 -> x0, local copies, waits for them, and re-layouts: 28.8 us -> none  [the longest x1 3.62 us: local(): back_out.reshape(devices * capacity, width)]
    all_to_all x4 -> x0, starting transfers between devices: 20.3 us -> none  [the longest x1 7.46 us: local(): lax.all_to_all(send_grad, 'expert', split_axis=0, concat_axis=0, tiled=True)]
  transfers between devices with their start and end apart: 4 -> 0, of which waited for: 4 -> 0; matrix products, arithmetic and copies ran while one was open for 18% -> 0% of each run, Pallas kernels for 0% -> 0%
where the time goes in v1:
time: 168 us
  Pallas kernels  149 us (89%)
  matrix products  12.2 us (7%)
  local copies, waits for them, and re-layouts  4.66 us (3%)
    pallas_call x1, Pallas kernels, local(): pl.pallas_call(functools.partial(kernel, n, cap, part, tile), out_shape=(...  149 us
    dot_general x3, matrix products, local(): lax.dot_general(a, b, TN, preferred_element_type=F32).astype(BF16)  12.2 us

profile of v1, /device:TPU:0, one launch (start us, length us, event | category | flops | bytes accessed | tf_op | source)
XLA Modules:
  0.0 167.9 jit_solution(17090953687801690885)
XLA Ops:
  0.6 1.4 copy.15.weight_col
  2.1 1.4 copy.14.idx_col
  3.5 148.8 %routed.1 = (bf16[192,2048]{1,0:T(8,128)(2,1)}, bf16[192,2048]{1,0:T(8,128)(2,1)}, f32[192,1]{1,0:T(8,128)}, bf16[384,2048]{1,0:T(8,128)(2,1)}, bf16[384,2048]{1...) custom-call(s32[1,192]{1,0:T(1,128)} %bitcast.20, ...), custom_call_target="tpu_custom_call" | custom-call | tf_op jit(solution)/shard_map/routed/pallas_call | solution.py:269
  152.4 1.6 reduce
  153.9 0.0 copy-start.3
  153.9 0.0 copy-start.5
  153.9 5.2 %fusion = bf16[1,2048,768]{2,1,0:T(8,128)(2,1)} fusion(bf16[384,2048]{1,0:T(8,128)(2,1)} %get-tuple-element.17, bf16[384,768]{1,0:T(8,128)(2,1)} %get-tuple-element.18), kind=kOutput, calls=%fused_computation.3 | convolution fusion | flops 1209532416 | bytes 5308416 | tf_op jit(solution)/shard_map/dot_general | solution.py:312
  159.1 0.0 copy-done.3
  159.1 0.0 copy-done.5
  159.1 0.0 copy-start.2
  159.1 0.0 copy-start.4
  159.2 3.5 %fusion.1 = bf16[1,2048,768]{2,1,0:T(8,128)(2,1)} fusion(bf16[384,2048]{1,0:T(8,128)(2,1)S(1)} %copy-done.3, bf16[384,768]{1,0:T(8,128)(2,1)S(1)} %copy-done.5), kind=kOutput, calls=%fused_computation.4 | convolution fusion | flops 1209532416 | bytes 5308416 | tf_op jit(solution)/shard_map/dot_general | solution.py:312
  162.7 0.0 copy-done.2
  162.7 0.0 copy-done.4
  162.7 0.0 copy-start.1
  162.7 0.0 copy-start
  162.7 3.5 %fusion.2 = bf16[1,768,2048]{2,1,0:T(8,128)(2,1)} fusion(bf16[384,768]{1,0:T(8,128)(2,1)S(1)} %copy-done.4, bf16[384,2048]{1,0:T(8,128)(2,1)S(1)} %copy-done.2), kind=kOutput, calls=%fused_computation.5 | convolution fusion | flops 1209532416 | bytes 5308416 | tf_op jit(solution)/shard_map/dot_general | solution.py:312
  166.2 0.0 copy-done.1
  166.2 0.9 copy.18
  167.1 0.0 copy-done
  167.1 0.9 copy.19
Async XLA Ops:
  153.9 5.2 %copy-start.3 = (bf16[384,2048]{1,0:T(8,128)(2,1)S(1)}, bf16[384,2048]{1,0:T(8,128)(2,1)}, u32[]{:S(2)}) copy-start(bf16[384,2048]{1,0:T(8,128)(2,1)} %get-tuple-element.17) | copy-start | bytes 4718596
  153.9 5.2 %copy-start.5 = (bf16[384,768]{1,0:T(8,128)(2,1)S(1)}, bf16[384,768]{1,0:T(8,128)(2,1)}, u32[]{:S(2)}) copy-start(bf16[384,768]{1,0:T(8,128)(2,1)} %get-tuple-element.19) | copy-start | bytes 1769476
  159.1 3.5 %copy-start.2 = (bf16[384,2048]{1,0:T(8,128)(2,1)S(1)}, bf16[384,2048]{1,0:T(8,128)(2,1)}, u32[]{:S(2)}) copy-start(bf16[384,2048]{1,0:T(8,128)(2,1)} %get-tuple-element.21) | copy-start | bytes 4718596
  159.1 3.5 %copy-start.4 = (bf16[384,768]{1,0:T(8,128)(2,1)S(1)}, bf16[384,768]{1,0:T(8,128)(2,1)}, u32[]{:S(2)}) copy-start(bf16[384,768]{1,0:T(8,128)(2,1)} %get-tuple-element.20) | copy-start | bytes 1769476
  162.7 3.5 %copy-start.1 = (bf16[192,2048]{1,0:T(8,128)(2,1)S(1)}, bf16[192,2048]{1,0:T(8,128)(2,1)}, u32[]{:S(2)}) copy-start(bf16[192,2048]{1,0:T(8,128)(2,1)} %get-tuple-element.28) | copy-start | bytes 2359300
  162.7 4.4 %copy-start = (bf16[192,2048]{1,0:T(8,128)(2,1)S(1)}, bf16[192,2048]{1,0:T(8,128)(2,1)}, u32[]{:S(2)}) copy-start(bf16[192,2048]{1,0:T(8,128)(2,1)} %get-tuple-element.29) | copy-start | bytes 2359300
